TPU v7x, 32 devices: a whole 2x2x4 slice. The times are simulated.
32 devices in a mesh: seq: 8 (over z, x), tp: 4 (over y, core).
Axes of the slice: x: 2, y: 2, z: 4, core: 2. Of those that a mesh axis runs over, the one named last changes fastest.
Arguments:
- tree_hidden: bfloat16 [16, 8192], P(None, 'seq'), may hold values from -6 to 6
- query_low: bfloat16 [16, 8192], P('seq', 'tp'), may hold values from -24 to 24
- key_tree_low: bfloat16 [16, 1024], P('seq', 'tp'), may hold values from -20 to 20
- value_tree_low: bfloat16 [16, 1024], P('seq', 'tp'), may hold values from -6 to 6
- cache_keys: bfloat16 [1, 8192, 8, 128], P(None, 'seq', 'tp'), may hold values from -40 to 40
- cache_values: bfloat16 [1, 8192, 8, 128], P(None, 'seq', 'tp'), may hold values from -6 to 6
- cache_lengths: int32 [1], replicated, may hold values from 1024 to 8192
- ancestors: int32 [1, 16, 16], replicated, may hold values from 0 to 1, as said below
- out_weight: bfloat16 [8192, 8192], P('tp', 'seq'), may hold values from -0.0625 to 0.0625
- norm_gain: float32 [8192], P('seq'), may hold values from 0.1 to 1.9
- w_query_up: bfloat16 [8192, 8192], P('seq', 'tp'), may hold values from -0.0625 to 0.0625
- w_key_up: bfloat16 [8192, 1024], P('seq', 'tp'), may hold values from -0.5 to 0.5
- w_value_up: bfloat16 [8192, 1024], P('seq', 'tp'), may hold values from -0.0625 to 0.0625
- retained_keys: bfloat16 [8, 512, 8, 128], P('seq', None, 'tp'), may hold values from -400 to 400
- retained_values: bfloat16 [8, 512, 8, 128], P('seq', None, 'tp'), may hold values from -6 to 6
- retained_index: int32 [8, 512, 8], P('seq', None, 'tp'), may hold values from 0 to 8191
Outputs:
- residual: float32 [16, 8192], P(None, 'seq')
- upper_heads: float32 [16, 8192], P('seq', 'tp')
Inputs may be any that keep to these rules, and one draw needn't show every extreme that they name: ancestors[r, i, j] is 1 when node j is node i or an ancestor of node i in request r's tree, else 0; node 0 is the root and every other node's parent has a lower number.
All inputs are finite; a program needn't handle non-finite values.
Results may differ from a plain program's by a relative error of at most 0.04.
Values may be sent and summed in bfloat16 or wider, within the bound.
A program may use at most 64 MiB of HBM per device.

v0:
```python
import functools

import jax
import jax.numpy as jnp
from jax import lax
from jax.experimental import pallas as pl
from jax.experimental.pallas import tpu as pltpu
from jax.sharding import PartitionSpec as P

MESH = pl.DeviceIdType.MESH
F32 = jnp.float32
BF16 = jnp.bfloat16
masked_score = -1e30
lowest_high = -1e29
norm_epsilon = 1e-05


def attend(queries, keys, values, allowed, scale):
    scores = lax.dot_general(
        queries, keys, (((1,), (1,)), ((), ())), preferred_element_type=F32
    ) * scale
    scores = jnp.where(allowed, scores, masked_score)
    high = jnp.maximum(jnp.max(scores, axis=1, keepdims=True), lowest_high)
    weights = jnp.exp(scores - high)
    total = jnp.sum(weights, axis=1, keepdims=True)
    blend = jnp.dot(weights.astype(BF16), values, preferred_element_type=F32)
    return blend, high, total


def kernel(
    sizes,
    lens_hbm,
    q_hbm,
    k_hbm,
    v_hbm,
    ck_hbm,
    cv_hbm,
    anc_hbm,
    ow_hbm,
    hid_hbm,
    gain_hbm,
    wk_hbm,
    wv_hbm,
    wq_hbm,
    ridx_hbm,
    rk_hbm,
    rv_hbm,
    res_ref,
    up_ref,
    lens_ref,
    q_ref,
    k_ref,
    v_ref,
    ck,
    cv,
    anc_ref,
    ow,
    hid_ref,
    gain_ref,
    wk,
    wv,
    wq,
    ridx_ref,
    rk,
    rv,
    form,
    low,
    part,
    gpart,
    heads,
    terms,
    proj,
    gproj,
    upper,
    upart,
    ugpart,
    load_sem,
    send_sem,
    recv_sem,
):
    S, T, R, own, kv, g, hd = sizes
    G = S // R
    M = S * own
    rows = own * g
    nodes = G * own
    scale = hd ** (-0.5)
    width = S * hid_ref.shape[1]
    me = lax.axis_index("seq")
    tp = lax.axis_index("tp")
    request = me // G
    base = request * G
    place = me - base

    barrier = pltpu.get_barrier_semaphore()
    for d in range(1, S):
        pl.semaphore_signal(
            barrier, inc=1, device_id={"seq": lax.rem(me + d, S)}, device_id_type=MESH
        )
    for d in range(1, T):
        pl.semaphore_signal(
            barrier, inc=1, device_id={"tp": lax.rem(tp + d, T)}, device_id_type=MESH
        )

    loads = []
    for i, (src, dst) in enumerate(
        (
            (q_hbm, q_ref),
            (k_hbm, k_ref),
            (v_hbm, v_ref),
            (ck_hbm, ck),
            (cv_hbm, cv),
            (anc_hbm, anc_ref),
            (ow_hbm, ow),
            (hid_hbm, hid_ref),
            (gain_hbm, gain_ref),
            (wk_hbm, wk),
            (wv_hbm, wv),
            (wq_hbm, wq),
            (ridx_hbm, ridx_ref),
            (rk_hbm, rk),
            (rv_hbm, rv),
            (lens_hbm, lens_ref),
        )
    ):
        copy = pltpu.make_async_copy(src, dst, load_sem.at[i])
        copy.start()
        loads.append(copy)

    sent = []

    def send(phase, d, src, dst, target):
        copy = pltpu.make_async_remote_copy(
            src_ref=src,
            dst_ref=dst,
            send_sem=send_sem.at[phase, d],
            recv_sem=recv_sem.at[phase, d],
            device_id=target,
            device_id_type=MESH,
        )
        copy.start()
        sent.append(copy)

    def arrive(phase, d, src, dst, target):
        pltpu.make_async_remote_copy(
            src_ref=src,
            dst_ref=dst,
            send_sem=send_sem.at[phase, d],
            recv_sem=recv_sem.at[phase, d],
            device_id=target,
            device_id_type=MESH,
        ).wait_recv()

    def peer(d):
        return lax.rem(me + d, S)

    def mate(d):
        return lax.rem(place + d, G)

    def tree_rows(block, j):
        return block[pl.ds(j, nodes, stride=g), :].astype(BF16)

    lanes = lax.broadcasted_iota(jnp.int32, (nodes * g, hd), 1)

    third = 32

    def pack_stats(stats):
        packed = jnp.zeros((nodes * g, hd), F32)
        spot = jnp.bitwise_and(lanes, third - 1)
        for k, (high, total) in enumerate(stats):
            packed = jnp.where(spot == 2 * k, high, packed)
            packed = jnp.where(spot == 2 * k + 1, total, packed)
        coarse = packed.astype(BF16).astype(F32)
        rest = packed - coarse
        middle = rest.astype(BF16).astype(F32)
        fine = rest - middle
        packed = jnp.where(lanes < third, coarse, jnp.where(lanes < 2 * third, middle, fine))
        return jnp.where(lanes < 3 * third, packed, 0.0).astype(BF16)

    def unpack_stats(block):
        packed = block.astype(F32)
        return (packed + pltpu.roll(packed, hd - third, 1)) + pltpu.roll(packed, hd - 2 * third, 1)

    def tree_part(own_queries, tree_block, tree_mask):
        return [
            attend(
                own_queries[k],
                tree_rows(tree_block, k),
                tree_rows(tree_block, kv + k),
                tree_mask,
                scale,
            )
            for k in range(kv)
        ]

    def finish(parts_ref, count, trees):
        stats = [unpack_stats(parts_ref[s, kv]) for s in range(count)]
        top = functools.reduce(jnp.maximum, stats)
        factors = [jnp.exp(x - top) for x in stats]
        done = []
        for k in range(kv):
            blend, high, total = trees[k]
            part_top = top[:, 2 * k : 2 * k + 1]
            highest = jnp.maximum(part_top, high)
            late = jnp.exp(high - highest)
            early = jnp.exp(part_top - highest)
            acc = jnp.zeros((rows, hd), F32)
            mass = jnp.zeros((rows, 1), F32)
            for s in range(count):
                factor = factors[s][:, 2 * k : 2 * k + 1]
                acc = acc + parts_ref[s, k].astype(F32) * factor
                mass = mass + stats[s][:, 2 * k + 1 : 2 * k + 2] * factor
            done.append((acc * early + blend * late) / (mass * early + total * late))
        return done

    form[kv] = jnp.zeros((M * g, hd), F32)
    for i in range(3):
        loads[i].wait()
    q_rows = q_ref[...].astype(F32)
    k_rows = k_ref[...].astype(F32)
    v_rows = v_ref[...].astype(F32)
    for k in range(kv):
        for j in range(g):
            h = k * g + j
            form[k, pl.ds(j, own, stride=g), :] = q_rows[:, h * hd : (h + 1) * hd]
        form[kv, pl.ds(k, own, stride=g), :] = k_rows[:, k * hd : (k + 1) * hd]
        form[kv, pl.ds(kv + k, own, stride=g), :] = v_rows[:, k * hd : (k + 1) * hd]
    for k in range(kv + 1):
        low[me, k] = form[k, :rows, :].astype(BF16)

    pl.semaphore_wait(barrier, S - 1 + T - 1)

    for d in range(1, S):
        own_q = low.at[me, pl.ds(0, kv)]
        send(0, d, own_q, own_q, {"seq": peer(d)})
    for d in range(1, S):
        own_kv = low.at[me, pl.ds(kv, 1)]
        send(2, d, own_kv, own_kv, {"seq": peer(d)})
    loads[3].wait()
    loads[4].wait()
    loads[5].wait()
    loads[15].wait()
    mask_rows = []
    node_start = place * own
    for r in range(own):
        row = anc_ref[request, pl.ds(node_start + r, 1), :]
        mask_rows.append(jnp.broadcast_to(row, (g, nodes)))
    tree_mask = jnp.concatenate(mask_rows, axis=0) > 0
    for d in range(1, S):
        source = peer(S - d)
        there = low.at[source, pl.ds(0, kv)]
        arrive(0, d, there, there, {"seq": source})

    columns = ck.shape[1]
    column = lax.broadcasted_iota(jnp.int32, (1, columns), 1)
    first = me * (columns // kv)

    def cache_request(r, carry):
        limit = (lens_ref[r] - first) * kv
        stats = []
        for k in range(kv):
            queries = low[pl.ds(r * G, G), k].reshape(nodes * g, hd)
            allowed = jnp.logical_and(
                jnp.bitwise_and(column, kv - 1) == k, column < limit
            )
            blend, high, total = attend(queries, ck[r], cv[r], allowed, scale)
            stats.append((high, total))
            for a in range(G):
                part[r * G + a, k] = blend[a * rows : (a + 1) * rows].astype(BF16)
        packed = pack_stats(stats)
        for a in range(G):
            part[r * G + a, kv] = packed[a * rows : (a + 1) * rows]
        return carry

    if R == 1:
        cache_request(0, 0)
    else:
        lax.fori_loop(0, R, cache_request, 0)
    for d in range(1, S):
        target = peer(d)
        send(1, d, part.at[target], gpart.at[me], {"seq": target})
    gpart[me] = part[me]
    for d in range(1, S):
        source = peer(S - d)
        there = low.at[source, pl.ds(kv, 1)]
        arrive(2, d, there, there, {"seq": source})
    form[kv, : nodes * g, :] = low[pl.ds(base, G), kv].reshape(nodes * g, hd).astype(F32)
    trees = tree_part([low[me, k] for k in range(kv)], form.at[kv], tree_mask)
    for d in range(1, S):
        source = peer(S - d)
        arrive(1, d, part.at[source], gpart.at[source], {"seq": source})

    done = finish(gpart, S, trees)
    for k in range(kv):
        heads[me, k] = done[k].astype(BF16)
    for d in range(1, S):
        send(3, d, heads.at[me], heads.at[me], {"seq": peer(d)})
    loads[6].wait()
    for d in range(1, S):
        source = peer(S - d)
        arrive(3, d, heads.at[source], heads.at[source], {"seq": source})

    for k in range(kv):
        form[k] = heads[:, k].reshape(M * g, hd).astype(F32)
    lower = jnp.concatenate(
        [
            form[k, pl.ds(j, M, stride=g), :].astype(BF16)
            for k in range(kv)
            for j in range(g)
        ],
        axis=1,
    )
    terms[tp] = jnp.dot(lower, ow[...], preferred_element_type=F32).astype(BF16)
    for d in range(1, T):
        send(4, d, terms.at[tp], terms.at[tp], {"tp": lax.rem(tp + d, T)})
    for i in range(7, 12):
        loads[i].wait()
    for d in range(1, T):
        source = lax.rem(tp + T - d, T)
        arrive(4, d, terms.at[source], terms.at[source], {"tp": source})
    residual = hid_ref[...].astype(F32)
    summed = terms[0].astype(F32)
    for t in range(1, T):
        summed = summed + terms[t].astype(F32)
    residual = residual + summed
    res_ref[...] = residual

    squares = jnp.broadcast_to(jnp.sum(residual * residual, axis=1, keepdims=True), (M, hd))
    coarse = squares.astype(BF16).astype(F32)
    scaled = (residual * gain_ref[...]).astype(BF16)
    query_terms = jnp.dot(scaled, wq[...], preferred_element_type=F32)
    key_terms = jnp.dot(scaled, wk[...], preferred_element_type=F32)
    value_terms = jnp.dot(scaled, wv[...], preferred_element_type=F32)
    form[kv] = jnp.zeros((M * g, hd), F32)
    for k in range(kv):
        for j in range(g):
            h = k * g + j
            form[k, pl.ds(j, M, stride=g), :] = query_terms[:, h * hd : (h + 1) * hd]
        form[kv, pl.ds(k, M, stride=g), :] = key_terms[:, k * hd : (k + 1) * hd]
        form[kv, pl.ds(kv + k, M, stride=g), :] = value_terms[:, k * hd : (k + 1) * hd]
    form[kv, pl.ds(2 * kv, M, stride=g), :] = coarse
    form[kv, pl.ds(2 * kv + 1, M, stride=g), :] = squares - coarse
    for s in range(S):
        for k in range(kv + 1):
            proj[s, k] = form[k, s * rows : (s + 1) * rows, :].astype(BF16)
    for d in range(1, S):
        target = peer(d)
        send(5, d, proj.at[target], gproj.at[me], {"seq": target})
    gproj[me] = proj[me]
    for d in range(1, S):
        source = peer(S - d)
        arrive(5, d, proj.at[source], gproj.at[source], {"seq": source})
    sums = []
    for k in range(kv + 1):
        total = gproj[0, k].astype(F32)
        for s in range(1, S):
            total = total + gproj[s, k].astype(F32)
        sums.append(total)
    inverses = []
    for r in range(own):
        at = r * g + 2 * kv
        square = sums[kv][at : at + 1, :] + sums[kv][at + 1 : at + 2, :]
        inverse = lax.rsqrt(square / width + norm_epsilon)
        inverses.append(jnp.broadcast_to(inverse, (g, hd)))
    inverse = jnp.concatenate(inverses, axis=0)

    own_queries = []
    for k in range(kv + 1):
        block = (sums[k] * inverse).astype(BF16)
        upper[place, k] = block
        own_queries.append(block)
    for d in range(1, G):
        own_q = upper.at[place, pl.ds(0, kv)]
        send(6, d, own_q, own_q, {"seq": base + mate(d)})
    for d in range(1, G):
        own_kv = upper.at[place, pl.ds(kv, 1)]
        send(8, d, own_kv, own_kv, {"seq": base + mate(d)})
    for i in range(12, 15):
        loads[i].wait()
    entries = rk.shape[0]
    chunk = min(hd, entries // kv)
    at_row = lax.broadcasted_iota(jnp.int32, (chunk, chunk * kv), 0)
    at_column = lax.broadcasted_iota(jnp.int32, (chunk, chunk * kv), 1)
    length_here = lens_ref[request]
    kept = []
    for k in range(kv):
        place_of = jnp.where(at_column == at_row * kv + k, 1.0, 0.0).astype(BF16)
        pieces = []
        for c in range(entries // kv // chunk):
            index_row = ridx_ref[k : k + 1, c * chunk : (c + 1) * chunk]
            flag = jnp.where(index_row < length_here, 1.0, 0.0)
            flag = jnp.broadcast_to(flag, (16, chunk)).astype(BF16)
            pieces.append(jnp.dot(flag, place_of, preferred_element_type=F32)[0:1, :])
        kept.append(jnp.concatenate(pieces, axis=1))
    for d in range(1, G):
        source = mate(G - d)
        there = upper.at[source, pl.ds(0, kv)]
        arrive(6, d, there, there, {"seq": base + source})

    stats = []
    for k in range(kv):
        allowed = kept[k] > 0.5
        queries = upper[:, k].reshape(nodes * g, hd)
        blend, high, total = attend(queries, rk[...], rv[...], allowed, scale)
        stats.append((high, total))
        for a in range(G):
            upart[a, k] = blend[a * rows : (a + 1) * rows].astype(BF16)
    packed = pack_stats(stats)
    for a in range(G):
        upart[a, kv] = packed[a * rows : (a + 1) * rows]
    for d in range(1, G):
        target = mate(d)
        send(7, d, upart.at[target], ugpart.at[place], {"seq": base + target})
    ugpart[place] = upart[place]
    for d in range(1, G):
        source = mate(G - d)
        there = upper.at[source, pl.ds(kv, 1)]
        arrive(8, d, there, there, {"seq": base + source})
    form[kv, : nodes * g, :] = upper[:, kv].reshape(nodes * g, hd).astype(F32)
    trees = tree_part(own_queries, form.at[kv], tree_mask)
    for d in range(1, G):
        source = mate(G - d)
        arrive(7, d, upart.at[source], ugpart.at[source], {"seq": base + source})
    done = finish(ugpart, G, trees)
    for k in range(kv):
        form[k, :rows, :] = done[k]
        for j in range(g):
            h = k * g + j
            up_ref[:, h * hd : (h + 1) * hd] = form[k, pl.ds(j, own, stride=g), :]
    for copy in sent:
        copy.wait_send()


def shards(
    tree_hidden,
    query_low,
    key_tree_low,
    value_tree_low,
    cache_keys,
    cache_values,
    cache_lengths,
    ancestors,
    out_weight,
    norm_gain,
    w_query_up,
    w_key_up,
    w_value_up,
    retained_keys,
    retained_values,
    retained_index,
):
    S = lax.axis_size("seq")
    T = lax.axis_size("tp")
    R, part, kv, hd = cache_keys.shape
    own, row_width = query_low.shape
    g = row_width // (kv * hd)
    G = S // R
    M = S * own
    rows = own * g
    features = tree_hidden.shape[1]
    entries = retained_keys.shape[1] * kv
    ck = cache_keys.reshape(R, part * kv, hd)
    cv = cache_values.reshape(R, part * kv, hd)
    rk = retained_keys.reshape(entries, hd)
    rv = retained_values.reshape(entries, hd)
    ridx = retained_index[0].T
    gain = norm_gain.reshape(1, features)
    vmem = pl.BlockSpec(memory_space=pltpu.VMEM)
    hbm = pl.BlockSpec(memory_space=pl.ANY)
    big = (
        query_low,
        key_tree_low,
        value_tree_low,
        ck,
        cv,
        ancestors,
        out_weight,
        tree_hidden,
        gain,
        w_key_up,
        w_value_up,
        w_query_up,
        ridx,
        rk,
        rv,
    )
    outs = pl.pallas_call(
        functools.partial(kernel, (S, T, R, own, kv, g, hd)),
        out_shape=(
            jax.ShapeDtypeStruct((M, features), F32),
            jax.ShapeDtypeStruct((own, row_width), F32),
        ),
        in_specs=[pl.BlockSpec(memory_space=pltpu.HBM)] + [hbm] * len(big),
        out_specs=(vmem, vmem),
        scratch_shapes=[pltpu.SMEM((R,), jnp.int32)]
        + [pltpu.VMEM(x.shape, x.dtype) for x in big]
        + [
            pltpu.VMEM((kv + 1, M * g, hd), F32),
            pltpu.VMEM((S, kv + 1, rows, hd), BF16),
            pltpu.VMEM((S, kv + 1, rows, hd), BF16),
            pltpu.VMEM((S, kv + 1, rows, hd), BF16),
            pltpu.VMEM((S, kv, rows, hd), BF16),
            pltpu.VMEM((T, M, features), BF16),
            pltpu.VMEM((S, kv + 1, rows, hd), BF16),
            pltpu.VMEM((S, kv + 1, rows, hd), BF16),
            pltpu.VMEM((G, kv + 1, rows, hd), BF16),
            pltpu.VMEM((G, kv + 1, rows, hd), BF16),
            pltpu.VMEM((G, kv + 1, rows, hd), BF16),
            pltpu.SemaphoreType.DMA((1 + len(big),)),
            pltpu.SemaphoreType.DMA((9, max(S, T))),
            pltpu.SemaphoreType.DMA((9, max(S, T))),
        ],
        compiler_params=pltpu.CompilerParams(
            collective_id=0, has_side_effects=True, vmem_limit_bytes=56 * 1024 * 1024
        ),
        name="two_layers",
    )(
        cache_lengths,
        *big,
    )

    def settle(a_ref, b_ref, c_ref, d_ref):
        c_ref[...] = a_ref[...]
        d_ref[...] = b_ref[...]

    return pl.pallas_call(
        settle,
        out_shape=tuple(jax.ShapeDtypeStruct(x.shape, x.dtype) for x in outs),
        in_specs=[vmem] * 2,
        out_specs=(vmem, vmem),
        name="settle",
    )(*outs)


def solution(mesh):
    return jax.shard_map(
        shards,
        mesh=mesh,
        in_specs=(
            P(None, "seq"),
            P("seq", "tp"),
            P("seq", "tp"),
            P("seq", "tp"),
            P(None, "seq", "tp", None),
            P(None, "seq", "tp", None),
            P(),
            P(),
            P("tp", "seq"),
            P("seq"),
            P("seq", "tp"),
            P("seq", "tp"),
            P("seq", "tp"),
            P("seq", None, "tp", None),
            P("seq", None, "tp", None),
            P("seq", None, "tp"),
        ),
        out_specs=(P(None, "seq"), P("seq", "tp")),
        check_vma=False,
    )
```

profile of v0, /device:TPU:0, one launch (start us, length us, event | category | flops | bytes accessed | tf_op | source)
XLA Modules:
  0.0 44.1 jit_solution(9597755383497335947)
XLA Ops:
  1.3 41.3 %two_layers.1 = (f32[16,1024]{1,0:T(8,128)}, f32[2,2048]{1,0:T(2,128)}) custom-call(s32[1]{0:T(128)S(6)} %copy.18.lens_hbm, bf16[2,2048]{1,0:T(2,128)(2,1)} %q_hbm.1, bf16[2,256]{1,0:T(2,128)(2,1)} %k_hbm.1, bf16[2,256]{1,0:T(2,128)(2,1)} %v_hbm.1, bf16[1,2048,128]{2,1,0:T(8,128)(2,1)} %bitcast.8, bf16[1,2048,128]{2,1,0:T(8,128)(2,1)} %bitcast.9, ...), custom_call_target="tpu_custom_call" | custom-call | tf_op jit(solution)/shard_map/two_layers/pallas_call | solution.py:486
  42.6 1.5 %settle.1 = (f32[16,1024]{1,0:T(8,128)}, f32[2,2048]{1,0:T(2,128)}) custom-call(f32[16,1024]{1,0:T(8,128)} %get-tuple-element.4.a_ref, f32[2,2048]{1,0:T(2,128)} %get-tuple-element.5.b_ref), custom_call_target="tpu_custom_call" | custom-call | tf_op jit(solution)/shard_map/settle/pallas_call | solution.py:525
where the time goes:
time: 44.3 us; the launch traced here: 44.1 us
  Pallas kernels  42.8 us (97%)
  between operations  1.29 us (3%)
    pallas_call x1, Pallas kernels, shards(): pl.pallas_call(functools.partial(kernel, (S, T, R, own, kv, g, hd)), out_...  41.3 us
    pallas_call x1, Pallas kernels, shards(): pl.pallas_call(settle, out_shape=tuple((jax.ShapeDtypeStruct(x.shape, x.d...  1.48 us

commit v1 on v0

v1 whole, which is shorter than its diff:
```python
import functools
import math

import jax
import jax.numpy as jnp
from jax import lax
from jax.experimental import pallas as pl
from jax.experimental.pallas import tpu as pltpu
from jax.sharding import PartitionSpec as P

MESH = pl.DeviceIdType.MESH
F32 = jnp.float32
BF16 = jnp.bfloat16
masked_score = -1e30
lowest_high = -1e29
norm_epsilon = 1e-05
last_last = (((1,), (1,)), ((), ()))


def contract_last(a, b):
    return lax.dot_general(a, b, last_last, preferred_element_type=F32)


def flip(index, bits):
    result = index
    bit = 1
    while bit <= bits:
        if bits & bit:
            result = result + (1 - 2 * lax.rem(lax.div(index, bit), 2)) * bit
        bit *= 2
    return result


def kernel(
    sizes,
    lens_hbm,
    q_hbm,
    k_hbm,
    v_hbm,
    ck_hbm,
    cv_hbm,
    anc_hbm,
    ow_hbm,
    hid_hbm,
    gain_hbm,
    ridx_hbm,
    rk_hbm,
    rv_hbm,
    wk_hbm,
    wv_hbm,
    wq_hbm,
    res_ref,
    up_ref,
    lens_ref,
    q_ref,
    k_ref,
    v_ref,
    ck,
    cv,
    anc_ref,
    ow,
    hid_ref,
    gain_ref,
    ridx_ref,
    rk,
    rv,
    weight,
    form,
    wide,
    ckeys,
    cvals,
    rkeys,
    rvals,
    bias_ref,
    low,
    part,
    gpart,
    tops,
    heads,
    terms,
    proj,
    gproj,
    square,
    gsquare,
    upper,
    upart,
    ugpart,
    load_sem,
    weight_sem,
    send_sem,
    recv_sem,
):
    S, T, R, own, kv, g, hd = sizes
    G = S // R
    H = G // 2
    M = S * own
    rows = own * g
    nodes = G * own
    lanes = nodes * g
    per_k = H // kv
    slab = hd // per_k
    qcols = kv * g * hd // H
    kcols = 2 * kv * hd // H
    hub_heads = qcols // hd
    scale = hd ** (-0.5)
    sharp = scale * math.log2(math.e)
    width = S * hid_ref.shape[1]
    half = hid_ref.shape[1] // 2
    me = lax.axis_index("seq")
    tp = lax.axis_index("tp")
    request = lax.div(me, G)
    base = request * G
    place = me - base
    first_hub = G // 4
    slot = place - first_hub
    is_hub = jnp.logical_and(place >= first_hub, place < first_hub + H)
    side = lax.div(place, G // 2)
    lane_of = lax.rem(place, per_k)

    def hub(r, c):
        return r * G + first_hub + c

    barrier = pltpu.get_barrier_semaphore()
    for d in range(1, S):
        pl.semaphore_signal(
            barrier, inc=1, device_id={"seq": flip(me, d)}, device_id_type=MESH
        )
    for d in range(1, T):
        pl.semaphore_signal(
            barrier, inc=1, device_id={"tp": flip(tp, d)}, device_id_type=MESH
        )

    loads = []
    for i, (src, dst) in enumerate(
        (
            (q_hbm, q_ref),
            (k_hbm, k_ref),
            (v_hbm, v_ref),
            (lens_hbm, lens_ref),
            (ck_hbm, ck),
            (cv_hbm, cv),
            (anc_hbm, anc_ref),
            (ow_hbm, ow),
            (rk_hbm, rk),
            (rv_hbm, rv),
            (ridx_hbm, ridx_ref),
            (hid_hbm, hid_ref),
            (gain_hbm, gain_ref),
        )
    ):
        copy = pltpu.make_async_copy(src, dst, load_sem.at[i])
        copy.start()
        loads.append(copy)
    weights = []
    for c in range(H):
        source, at = (wk_hbm, c) if c < H // 2 else (wv_hbm, c - H // 2)
        for i, (src, dst) in enumerate(
            (
                (wq_hbm.at[:, pl.ds(c * qcols, qcols)], weight.at[c, :, pl.ds(0, qcols)]),
                (source.at[:, pl.ds(at * kcols, kcols)], weight.at[c, :, pl.ds(qcols, kcols)]),
            )
        ):
            copy = pltpu.make_async_copy(src, dst, weight_sem.at[c, i])
            copy.start()
            weights.append(copy)

    sent = []

    def send(phase, at, src, dst, to, target, when=None):
        copy = pltpu.make_async_remote_copy(
            src_ref=src,
            dst_ref=dst,
            send_sem=send_sem.at[phase, at],
            recv_sem=recv_sem.at[phase, to],
            device_id=target,
            device_id_type=MESH,
        )
        if when is None:
            copy.start()
        else:
            pl.when(when)(copy.start)
        sent.append((when, copy))

    def arrive(phase, source, there, target, when=None):
        copy = pltpu.make_async_remote_copy(
            src_ref=there,
            dst_ref=there,
            send_sem=send_sem.at[phase, 0],
            recv_sem=recv_sem.at[phase, source],
            device_id=target,
            device_id_type=MESH,
        )
        if when is None:
            copy.wait_recv()
        else:
            pl.when(when)(copy.wait_recv)

    row_a = lax.broadcasted_iota(jnp.int32, (lanes, lanes), 0)
    col_a = lax.broadcasted_iota(jnp.int32, (lanes, lanes), 1)

    def one_hot(where):
        return jnp.where(where, 1.0, 0.0).astype(BF16)

    form[kv] = jnp.zeros(form.shape[1:], F32)
    for i in range(3):
        loads[i].wait()
    q_rows = q_ref[...].astype(F32)
    k_rows = k_ref[...].astype(F32)
    v_rows = v_ref[...].astype(F32)
    for k in range(kv):
        for j in range(g):
            h = k * g + j
            form[k, pl.ds(j, own, stride=g), :] = q_rows[:, h * hd : (h + 1) * hd]
        form[kv, pl.ds(k, own, stride=g), :] = k_rows[:, k * hd : (k + 1) * hd]
        form[kv, pl.ds(kv + k, own, stride=g), :] = v_rows[:, k * hd : (k + 1) * hd]
    for k in range(kv + 1):
        low[me, k] = form[k, :rows, :].astype(BF16)

    pl.semaphore_wait(barrier, S - 1 + T - 1)

    for d in reversed(range(1, S)):
        own_q = low.at[me, pl.ds(0, kv)]
        send(0, d, own_q, own_q, me, {"seq": flip(me, d)})
    for c in range(H):
        own_kv = low.at[me, pl.ds(kv, 1)]
        target = hub(request, c)
        send(2, c, own_kv, own_kv, me, {"seq": target}, target != me)

    for i in range(3, 7):
        loads[i].wait()
    columns = ckeys.shape[2]
    first = me * columns
    position = lax.broadcasted_iota(jnp.int32, (columns, hd), 0) + first
    for r in range(R):
        wide[: columns * kv] = ck[r].astype(F32)
        allowed = jnp.where(position < lens_ref[r], 0.0, masked_score).astype(BF16)
        for k in range(kv):
            ckeys[r, k, :, :hd] = wide[pl.ds(k, columns, stride=kv), :].astype(BF16)
            ckeys[r, k, :, hd:] = allowed
        wide[: columns * kv] = cv[r].astype(F32)
        for k in range(kv):
            cvals[r, k, :hd, :] = wide[pl.ds(k, columns, stride=kv), :].T.astype(BF16)
            cvals[r, k, hd:, :] = jnp.ones((cvals.shape[2] - hd, columns), BF16)

    lead = one_hot(lax.broadcasted_iota(jnp.int32, (lanes, hd), 1) == 0)
    row_s = lax.broadcasted_iota(jnp.int32, (16, lanes), 0)
    for d in range(1, S):
        source = flip(me, d)
        arrive(0, source, low.at[source, pl.ds(0, kv)], {"seq": source})

    for r in range(R):
        for step in range(kv):
            k = lax.rem(side + kv - 1 - step, kv)
            queries = low[pl.ds(r * G, G), k].reshape(lanes, hd)
            queries = jnp.concatenate([queries, lead], axis=1)
            scores = contract_last(ckeys[r, k], queries)
            high = jnp.maximum(jnp.max(scores, axis=0, keepdims=True), lowest_high)
            high = high.astype(BF16).astype(F32)
            mass = jnp.exp2((scores - high) * sharp).astype(BF16)
            blend = jnp.dot(cvals[r, k], mass, preferred_element_type=F32)
            total = blend[hd : hd + 1]
            coarse = total.astype(BF16).astype(F32)
            stats = jnp.where(row_s == 1, coarse, jnp.where(row_s == 2, total - coarse, 0.0))
            stats = jnp.where(row_s == 0, high, stats).astype(BF16)
            for h in range(per_k):
                part[r, k * per_k + h, :slab, :] = blend[h * slab : (h + 1) * slab].astype(BF16)
                part[r, k * per_k + h, slab:, :] = stats
            for d in reversed(range(per_k)):
                c = k * per_k + lax.rem(lane_of + d, per_k)
                target = hub(r, c)
                send(
                    1,
                    (r * kv + step) * per_k + d,
                    part.at[r, c],
                    gpart.at[me],
                    me,
                    {"seq": target},
                    target != me,
                )

    @pl.when(is_hub)
    def _():
        k = lax.div(slot, per_k)
        part_of = lax.rem(slot, per_k)
        ancestry = anc_ref[request].astype(F32).astype(BF16)
        spread = one_hot(
            lax.div(lax.broadcasted_iota(jnp.int32, (lanes, nodes), 0), g)
            == lax.broadcasted_iota(jnp.int32, (lanes, nodes), 1)
        )
        mask = jnp.dot(spread, ancestry, preferred_element_type=F32).astype(BF16)
        small = one_hot(
            lax.broadcasted_iota(jnp.int32, (nodes, nodes), 0)
            == lax.broadcasted_iota(jnp.int32, (nodes, nodes), 1)
        )
        mask = contract_last(small, mask)
        for d in range(1, G):
            source = base + flip(place, d)
            arrive(2, source, low.at[source, pl.ds(kv, 1)], {"seq": source})
        form[kv, :lanes, :] = low[pl.ds(base, G), kv].reshape(lanes, hd).astype(F32)
        keys = form[kv, pl.ds(k, nodes, stride=g), :].astype(BF16)
        values = form[kv, pl.ds(kv + k, nodes, stride=g), :].astype(BF16)
        scores = contract_last(keys, low[pl.ds(base, G), k].reshape(lanes, hd))
        scores = jnp.where(mask > 0.5, scores, masked_score)
        near_high = jnp.max(scores, axis=0, keepdims=True)
        mass = jnp.exp2((scores - near_high) * sharp)
        near_total = jnp.sum(mass, axis=0, keepdims=True)
        turned = contract_last(one_hot(row_a == col_a)[:hd, :hd], values).astype(BF16)
        wide[:hd] = jnp.dot(turned, mass.astype(BF16), preferred_element_type=F32)
        near = wide[pl.ds(pl.multiple_of(part_of * slab, slab), slab), :]
        gpart[me] = part[request, slot]
        for d in range(1, S):
            source = flip(me, d)
            arrive(1, source, gpart.at[source], {"seq": source})
        for s in range(S):
            tops[s * 16 : (s + 1) * 16] = gpart[s, slab:].astype(F32)
        highs = tops[pl.ds(0, S, stride=16), :]
        totals = tops[pl.ds(1, S, stride=16), :] + tops[pl.ds(2, S, stride=16), :]
        top = jnp.maximum(jnp.max(highs, axis=0, keepdims=True), near_high)
        factors = jnp.exp2((highs - top) * sharp)
        late = jnp.exp2((near_high - top) * sharp)
        total = jnp.sum(factors * totals, axis=0, keepdims=True) + near_total * late
        acc = near * late
        for s in range(S):
            acc = acc + gpart[s, :slab].astype(F32) * factors[s : s + 1]
        heads[request, slot] = (acc * (1.0 / total)).astype(BF16)

    for d in reversed(range(1, S)):
        done = heads.at[request, slot]
        send(3, d, done, done, me, {"seq": flip(me, d)}, is_hub)

    entries = rkeys.shape[1]
    for i in range(7, 11):
        loads[i].wait()
    wide[: entries * kv] = rk[...].astype(F32)
    for k in range(kv):
        rkeys[k] = wide[pl.ds(k, entries, stride=kv), :].astype(BF16)
    wide[: entries * kv] = rv[...].astype(F32)
    for k in range(kv):
        rvals[k, :, :hd] = wide[pl.ds(k, entries, stride=kv), :].astype(BF16)
        rvals[k, :, hd:] = jnp.ones((entries, hd), BF16)
        kept = jnp.where(ridx_ref[k : k + 1, :] < lens_ref[request], 0.0, masked_score)
        bias_ref[k] = jnp.broadcast_to(kept, bias_ref.shape[1:])
    mask_rows = []
    for r in range(own):
        row = anc_ref[request, pl.ds(place * own + r, 1), :]
        mask_rows.append(jnp.broadcast_to(row, (g, nodes)))
    tree_mask = jnp.concatenate(mask_rows, axis=0) > 0
    order = one_hot(
        jnp.logical_and(
            lax.rem(row_a, nodes) == lax.div(col_a, g),
            lax.div(row_a, nodes) == lax.rem(col_a, g),
        )
    )

    summed = None
    for step in range(kv):
        k = lax.rem(side + step, kv)
        lower = []
        for r in range(R):
            for d in range(per_k):
                c = k * per_k + lax.rem(lane_of + d, per_k)
                source = hub(r, c)
                arrive(3, source, heads.at[r, c], {"seq": source}, source != me)
            turned = heads[r, pl.ds(k * per_k, per_k)].reshape(hd, lanes)
            turned = contract_last(order, turned).astype(BF16)
            lower.append(
                jnp.concatenate(
                    [turned[j * nodes : (j + 1) * nodes] for j in range(g)], axis=1
                )
            )
        lower = lower[0] if R == 1 else jnp.concatenate(lower, axis=0)
        depth = g * hd
        start = pl.multiple_of(k * depth, depth)
        if step < kv - 1:
            more = jnp.dot(lower, ow[pl.ds(start, depth), :], preferred_element_type=F32)
            summed = more if summed is None else summed + more
        else:
            for p in range(2):
                more = jnp.dot(
                    lower,
                    ow[pl.ds(start, depth), p * half : (p + 1) * half],
                    preferred_element_type=F32,
                )
                if summed is not None:
                    more = more + summed[:, p * half : (p + 1) * half]
                terms[tp, p] = more.astype(BF16)
                for d in reversed(range(1, T)):
                    mine = terms.at[tp, p]
                    send(4, p * T + d, mine, mine, p * T + tp, {"tp": flip(tp, d)})
    loads[11].wait()
    loads[12].wait()
    residual = []
    for p in range(2):
        for d in range(1, T):
            source = flip(tp, d)
            arrive(4, p * T + source, terms.at[source, p], {"tp": source})
        summed = terms[0, p].astype(F32)
        for t in range(1, T):
            summed = summed + terms[t, p].astype(F32)
        residual.append(hid_ref[:, p * half : (p + 1) * half].astype(F32) + summed)
    residual = jnp.concatenate(residual, axis=1)

    squares = jnp.broadcast_to(jnp.sum(residual * residual, axis=1, keepdims=True), (M, hd))
    coarse = squares.astype(BF16).astype(F32)
    lane = lax.broadcasted_iota(jnp.int32, (M, hd), 1)
    squares = jnp.where(lane < hd // 2, coarse, squares - coarse).astype(BF16)
    for r in range(R):
        square[r] = squares[r * nodes : (r + 1) * nodes]
        for c in range(H):
            target = hub(r, c)
            send(
                9, r * H + c, square.at[r], gsquare.at[me], me, {"seq": target}, target != me
            )
    for copy in weights:
        copy.wait()
    scaled = (residual * gain_ref[...]).astype(BF16)
    for step in range(kv):
        for d in reversed(range(per_k)):
            c = lax.rem(side + kv - 1 - step, kv) * per_k + lax.rem(lane_of + d, per_k)
            out = jnp.dot(scaled, weight[c], preferred_element_type=F32).astype(BF16)
            for r in range(R):
                proj[r, c] = out[r * nodes : (r + 1) * nodes]
                target = hub(r, c)
                send(
                    5,
                    (r * kv + step) * per_k + d,
                    proj.at[r, c],
                    gproj.at[me],
                    me,
                    {"seq": target},
                    target != me,
                )
    res_ref[...] = residual

    @pl.when(is_hub)
    def _():
        gsquare[me] = square[request]
        gproj[me] = proj[request, slot]
        for d in range(1, S):
            source = flip(me, d)
            arrive(9, source, gsquare.at[source], {"seq": source})
        total = gsquare[0].astype(F32)
        for s in range(1, S):
            total = total + gsquare[s].astype(F32)
        total = total + pltpu.roll(total, hd // 2, 1)
        inverse = lax.rsqrt(total / width + norm_epsilon)
        for d in range(1, S):
            source = flip(me, d)
            arrive(5, source, gproj.at[source], {"seq": source})
        for t in range((qcols + kcols) // hd):
            at = slice(t * hd, (t + 1) * hd)
            total = gproj[0, :, at].astype(F32)
            for s in range(1, S):
                total = total + gproj[s, :, at].astype(F32)
            upper[slot, :, at] = (total * inverse).astype(BF16)

    for d in reversed(range(1, G)):
        mine = upper.at[slot]
        send(6, d, mine, mine, me, {"seq": base + flip(place, d)}, is_hub)

    spot = lax.broadcasted_iota(jnp.int32, (lanes, hd), 1)
    third = hd // 4

    def pack_stats(high, total):
        packed = jnp.where(jnp.bitwise_and(spot, 1) == 0, high, total)
        coarse = packed.astype(BF16).astype(F32)
        rest = packed - coarse
        middle = rest.astype(BF16).astype(F32)
        fine = rest - middle
        packed = jnp.where(spot < third, coarse, jnp.where(spot < 2 * third, middle, fine))
        return jnp.where(spot < 3 * third, packed, 0.0)

    def unpack_stats(block):
        packed = block.astype(F32)
        return (packed + pltpu.roll(packed, hd - third, 1)) + pltpu.roll(
            packed, hd - 2 * third, 1
        )

    pick = one_hot(
        jnp.logical_and(
            lax.div(lax.broadcasted_iota(jnp.int32, (rows, lanes), 0), g) + place * own
            == lax.rem(lax.broadcasted_iota(jnp.int32, (rows, lanes), 1), nodes),
            lax.rem(lax.broadcasted_iota(jnp.int32, (rows, lanes), 0), g)
            == lax.div(lax.broadcasted_iota(jnp.int32, (rows, lanes), 1), nodes),
        )
    )

    def upper_queries(k):
        tiles = []
        for j in range(g):
            tile = upper[k * per_k + j // hub_heads]
            tiles.append(tile[:, (j % hub_heads) * hd : (j % hub_heads + 1) * hd])
        return jnp.concatenate(tiles, axis=0)

    for step in range(kv):
        k = lax.rem(side + step, kv)
        for d in range(per_k):
            c = k * per_k + lax.rem(lane_of + d, per_k)
            source = hub(request, c)
            arrive(6, source, upper.at[c], {"seq": source}, source != me)
        scores = contract_last(upper_queries(k), rkeys[k]) + bias_ref[k, 0:1, :]
        high = jnp.maximum(jnp.max(scores, axis=1, keepdims=True), lowest_high)
        mass = jnp.exp2((scores - high) * sharp).astype(BF16)
        blend = jnp.dot(mass, rvals[k], preferred_element_type=F32)
        form[0, :lanes, :] = blend[:, :hd]
        form[1, :lanes, :] = pack_stats(high, blend[:, hd:])
        for a in range(G):
            for i in range(2):
                tile = [form[i, pl.ds(a * own + b, g, stride=nodes), :] for b in range(own)]
                upart[a, k, i * rows : (i + 1) * rows, :] = jnp.concatenate(tile, axis=0).astype(
                    BF16
                )
        for d in reversed(range(1, G)):
            target = flip(place, d)
            send(
                7,
                step * S + d,
                upart.at[target, k],
                ugpart.at[place, k],
                step * S + place,
                {"seq": base + target},
            )
    ugpart[place] = upart[place]

    trees = []
    for k in range(kv):
        queries = jnp.dot(pick, upper_queries(k), preferred_element_type=F32).astype(BF16)
        keys = upper[(k * hd) // kcols][:, qcols:]
        values = upper[H // 2 + (k * hd) // kcols][:, qcols:]
        scores = jnp.where(tree_mask, contract_last(queries, keys), masked_score)
        high = jnp.max(scores, axis=1, keepdims=True)
        mass = jnp.exp2((scores - high) * sharp)
        total = jnp.sum(mass, axis=1, keepdims=True)
        trees.append((jnp.dot(mass.astype(BF16), values, preferred_element_type=F32), high, total))
    for step in range(kv):
        for d in range(1, G):
            source = flip(place, d)
            k = lax.rem(lax.div(source, G // 2) + step, kv)
            arrive(7, step * S + source, ugpart.at[source, k], {"seq": base + source})
    for k in range(kv):
        blend, high, total = trees[k]
        stats = [unpack_stats(ugpart[s, k, rows:]) for s in range(G)]
        top = jnp.maximum(functools.reduce(jnp.maximum, stats)[:, 0:1], high)
        late = jnp.exp2((high - top) * sharp)
        acc = blend * late
        whole = total * late
        mass = jnp.zeros((rows, hd), F32)
        for s in range(G):
            factor = jnp.exp2((stats[s] - top) * sharp)
            acc = acc + ugpart[s, k, :rows].astype(F32) * factor[:, 0:1]
            mass = mass + pltpu.roll(stats[s], hd - 1, 1) * factor
        form[k, :rows, :] = acc / (whole + mass[:, 0:1])
        for j in range(g):
            h = k * g + j
            up_ref[:, h * hd : (h + 1) * hd] = form[k, pl.ds(j, own, stride=g), :]
    for when, copy in sent:
        if when is None:
            copy.wait_send()
        else:
            pl.when(when)(copy.wait_send)


def shards(
    tree_hidden,
    query_low,
    key_tree_low,
    value_tree_low,
    cache_keys,
    cache_values,
    cache_lengths,
    ancestors,
    out_weight,
    norm_gain,
    w_query_up,
    w_key_up,
    w_value_up,
    retained_keys,
    retained_values,
    retained_index,
):
    S = lax.axis_size("seq")
    T = lax.axis_size("tp")
    R, part, kv, hd = cache_keys.shape
    own, row_width = query_low.shape
    g = row_width // (kv * hd)
    G = S // R
    M = S * own
    rows = own * g
    features = tree_hidden.shape[1]
    entries = retained_keys.shape[1] * kv
    ck = cache_keys.reshape(R, part * kv, hd)
    cv = cache_values.reshape(R, part * kv, hd)
    rk = retained_keys.reshape(entries, hd)
    rv = retained_values.reshape(entries, hd)
    ridx = retained_index[0].T
    gain = norm_gain.reshape(1, features)
    vmem = pl.BlockSpec(memory_space=pltpu.VMEM)
    hbm = pl.BlockSpec(memory_space=pl.ANY)
    H = G // 2
    columns = part
    big = (
        query_low,
        key_tree_low,
        value_tree_low,
        ck,
        cv,
        ancestors,
        out_weight,
        tree_hidden,
        gain,
        ridx,
        rk,
        rv,
    )
    cols = (kv * g * hd + 2 * kv * hd) // H
    nodes = G * own
    lanes = nodes * g
    slab = hd * kv // H
    outs = pl.pallas_call(
        functools.partial(kernel, (S, T, R, own, kv, g, hd)),
        out_shape=(
            pltpu.VMEM((M, features), F32),
            pltpu.VMEM((own, row_width), F32),
        ),
        in_specs=[hbm] * (4 + len(big)),
        out_specs=(vmem, vmem),
        scratch_shapes=[pltpu.SMEM((R,), jnp.int32)]
        + [pltpu.VMEM(x.shape, x.dtype) for x in big]
        + [
            pltpu.VMEM((H, features, cols), BF16),
            pltpu.VMEM((kv + 1, lanes, hd), F32),
            pltpu.VMEM((max(columns * kv, entries), hd), F32),
            pltpu.VMEM((R, kv, columns, 2 * hd), BF16),
            pltpu.VMEM((R, kv, hd + 16, columns), BF16),
            pltpu.VMEM((kv, entries // kv, hd), BF16),
            pltpu.VMEM((kv, entries // kv, 2 * hd), BF16),
            pltpu.VMEM((kv, 8, entries // kv), F32),
            pltpu.VMEM((S, kv + 1, rows, hd), BF16),
            pltpu.VMEM((R, H, slab + 16, lanes), BF16),
            pltpu.VMEM((S, slab + 16, lanes), BF16),
            pltpu.VMEM((S * 16, lanes), F32),
            pltpu.VMEM((R, H, slab, lanes), BF16),
            pltpu.VMEM((T, 2, M, features // 2), BF16),
            pltpu.VMEM((R, H, nodes, cols), BF16),
            pltpu.VMEM((S, nodes, cols), BF16),
            pltpu.VMEM((R, nodes, hd), BF16),
            pltpu.VMEM((S, nodes, hd), BF16),
            pltpu.VMEM((H, nodes, cols), BF16),
            pltpu.VMEM((G, kv, 2 * rows, hd), BF16),
            pltpu.VMEM((G, kv, 2 * rows, hd), BF16),
            pltpu.SemaphoreType.DMA((1 + len(big),)),
            pltpu.SemaphoreType.DMA((H, 2)),
            pltpu.SemaphoreType.DMA((10, 2 * max(S, T))),
            pltpu.SemaphoreType.DMA((10, 2 * max(S, T))),
        ],
        compiler_params=pltpu.CompilerParams(
            collective_id=0, has_side_effects=True, vmem_limit_bytes=56 * 1024 * 1024
        ),
        name="two_layers",
    )(
        cache_lengths,
        *big,
        w_key_up,
        w_value_up,
        w_query_up,
    )

    def settle(a_ref, b_ref, c_ref, d_ref):
        c_ref[...] = a_ref[...]
        d_ref[...] = b_ref[...]

    return pl.pallas_call(
        settle,
        out_shape=tuple(jax.ShapeDtypeStruct(x.shape, x.dtype) for x in outs),
        in_specs=[vmem] * 2,
        out_specs=(vmem, vmem),
        name="settle",
    )(*[pltpu.with_memory_space_constraint(x, pltpu.VMEM) for x in outs])


def solution(mesh):
    return jax.shard_map(
        shards,
        mesh=mesh,
        in_specs=(
            P(None, "seq"),
            P("seq", "tp"),
            P("seq", "tp"),
            P("seq", "tp"),
            P(None, "seq", "tp", None),
            P(None, "seq", "tp", None),
            P(),
            P(),
            P("tp", "seq"),
            P("seq"),
            P("seq", "tp"),
            P("seq", "tp"),
            P("seq", "tp"),
            P("seq", None, "tp", None),
            P("seq", None, "tp", None),
            P("seq", None, "tp"),
        ),
        out_specs=(P(None, "seq"), P("seq", "tp")),
        check_vma=False,
    )
```

time: 44.3 us -> 41.7 us (0.941)
  Pallas kernels: 42.8 us -> 40.2 us
    pallas_call x1, Pallas kernels: 41.3 us -> 39.6 us  [shards(): pl.pallas_call(functools.partial(kernel, (S, T, R, own, kv, g, hd)), out_...]
    pallas_call x1, Pallas kernels: 1.48 us -> 0.64 us  [shards(): pl.pallas_call(settle, out_shape=tuple((jax.ShapeDtypeStruct(x.shape, x.d...]
where the time goes in v1:
time: 41.7 us; the launch traced here: 41.5 us
  Pallas kernels  40.2 us (96%)
  between operations  1.29 us (3%)
    pallas_call x1, Pallas kernels, shards(): pl.pallas_call(functools.partial(kernel, (S, T, R, own, kv, g, hd)), out_...  39.6 us

profile of v1, /device:TPU:0, one launch (start us, length us, event | category | flops | bytes accessed | tf_op | source)
XLA Modules:
  0.0 41.5 jit_solution(6025665125542611100)
XLA Ops:
  1.3 39.6 %two_layers.1 = (f32[16,1024]{1,0:T(8,128)S(1)}, f32[2,2048]{1,0:T(2,128)S(1)}) custom-call(s32[1]{0:T(128)S(6)} %copy.18.lens_hbm, bf16[2,2048]{1,0:T(2,128)(2,1)} %q_hbm.1, bf16[2,256]{1,0:T(2,128)(2,1)} %k_hbm.1, bf16[2,256]{1,0:T(2,128)(2,1)} %v_hbm.1, bf16[1,2048,128]{2,1,0:T(8,128)(2,1)} %bitcast.8, bf16[1,2048,128]{2,1,0:T(8,128)(2,1)} %bitcast.9, ...), custom_call_target="tpu_custom_call" | custom-call | tf_op jit(solution)/shard_map/two_layers/pallas_call | solution.py:619
  40.8 0.6 %settle.1 = (f32[16,1024]{1,0:T(8,128)}, f32[2,2048]{1,0:T(2,128)}) custom-call(f32[16,1024]{1,0:T(8,128)S(1)} %get-tuple-element.4.a_ref, f32[2,2048]{1,0:T(2,128)S(1)} %get-tuple-element.5.b_ref), custom_call_target="tpu_custom_call" | custom-call | tf_op jit(solution)/shard_map/settle/pallas_call | solution.py:672

commit v2 on v1

--- a/solution.py
+++ b/solution.py
@@ -21,14 +21,37 @@
     return lax.dot_general(a, b, last_last, preferred_element_type=F32)
 
 
-def flip(index, bits):
-    result = index
+def bits_of(index, count):
+    found = []
     bit = 1
-    while bit <= bits:
-        if bits & bit:
-            result = result + (1 - 2 * lax.rem(lax.div(index, bit), 2)) * bit
+    while 2 * bit < count:
         bit *= 2
+    while bit and count > 1:
+        there = jnp.where(index >= bit, 1, 0)
+        index = index - there * bit
+        found.append((bit, there))
+        bit //= 2
+    return found
+
+
+def flips(index, count):
+    steps = [(bit, (1 - 2 * there) * bit) for bit, there in bits_of(index, count)]
+    result = []
+    for d in range(count):
+        other = index
+        for bit, step in steps:
+            if d & bit:
+                other = other + step
+        result.append(other)
     return result
+
+
+def turn(index, step, count):
+    if step % count == 0:
+        return index
+    if count == 2:
+        return 1 - index
+    return lax.rem(index + step, count)
 
 
 def kernel(
@@ -108,14 +131,17 @@
     half = hid_ref.shape[1] // 2
     me = lax.axis_index("seq")
     tp = lax.axis_index("tp")
-    request = lax.div(me, G)
+    request = 0 if R == 1 else lax.div(me, G)
     base = request * G
     place = me - base
+    peers = flips(me, S)
+    mates = flips(place, G)
+    twins = flips(tp, T)
     first_hub = G // 4
     slot = place - first_hub
     is_hub = jnp.logical_and(place >= first_hub, place < first_hub + H)
-    side = lax.div(place, G // 2)
-    lane_of = lax.rem(place, per_k)
+    side = jnp.where(place >= G // 2, 1, 0)
+    lane_of = bits_of(place, G)[-1][1] if per_k == 2 else lax.rem(place, per_k)
 
     def hub(r, c):
         return r * G + first_hub + c
@@ -123,11 +149,11 @@
     barrier = pltpu.get_barrier_semaphore()
     for d in range(1, S):
         pl.semaphore_signal(
-            barrier, inc=1, device_id={"seq": flip(me, d)}, device_id_type=MESH
+            barrier, inc=1, device_id={"seq": peers[d]}, device_id_type=MESH
         )
     for d in range(1, T):
         pl.semaphore_signal(
-            barrier, inc=1, device_id={"tp": flip(tp, d)}, device_id_type=MESH
+            barrier, inc=1, device_id={"tp": twins[d]}, device_id_type=MESH
         )
 
     loads = []
@@ -151,49 +177,57 @@
         copy = pltpu.make_async_copy(src, dst, load_sem.at[i])
         copy.start()
         loads.append(copy)
-    weights = []
     for c in range(H):
         source, at = (wk_hbm, c) if c < H // 2 else (wv_hbm, c - H // 2)
-        for i, (src, dst) in enumerate(
-            (
+        for src, dst in (
                 (wq_hbm.at[:, pl.ds(c * qcols, qcols)], weight.at[c, :, pl.ds(0, qcols)]),
                 (source.at[:, pl.ds(at * kcols, kcols)], weight.at[c, :, pl.ds(qcols, kcols)]),
-            )
         ):
-            copy = pltpu.make_async_copy(src, dst, weight_sem.at[c, i])
-            copy.start()
-            weights.append(copy)
-
-    sent = []
-
-    def send(phase, at, src, dst, to, target, when=None):
-        copy = pltpu.make_async_remote_copy(
+            pltpu.make_async_copy(src, dst, weight_sem).start()
+
+    def remote(phase, src, dst, at, target):
+        return pltpu.make_async_remote_copy(
             src_ref=src,
             dst_ref=dst,
-            send_sem=send_sem.at[phase, at],
-            recv_sem=recv_sem.at[phase, to],
-            device_id=target,
+            send_sem=send_sem.at[phase],
+            recv_sem=recv_sem.at[at],
+            device_id={"seq": target},
             device_id_type=MESH,
         )
+
+    def send(phase, src, dst, at, target, when=None):
+        copy = remote(phase, src, dst, at, target)
         if when is None:
             copy.start()
         else:
             pl.when(when)(copy.start)
-        sent.append((when, copy))
-
-    def arrive(phase, source, there, target, when=None):
-        copy = pltpu.make_async_remote_copy(
-            src_ref=there,
-            dst_ref=there,
-            send_sem=send_sem.at[phase, 0],
-            recv_sem=recv_sem.at[phase, source],
-            device_id=target,
+
+    def send_twin(phase, src, dst, at, target):
+        pltpu.make_async_remote_copy(
+            src_ref=src,
+            dst_ref=dst,
+            send_sem=send_sem.at[phase],
+            recv_sem=recv_sem.at[at],
+            device_id={"tp": target},
             device_id_type=MESH,
-        )
+        ).start()
+
+    def arrive(at, block, when=None):
+        copy = remote(0, block, block, at, peers[1])
         if when is None:
             copy.wait_recv()
         else:
             pl.when(when)(copy.wait_recv)
+
+    def gone(phase, block, when=None):
+        copy = remote(phase, block, block, 0, peers[1])
+        if when is None:
+            copy.wait_send()
+        else:
+            pl.when(when)(copy.wait_send)
+
+    at_heads = 8
+    at_upper = at_heads + R * H
 
     row_a = lax.broadcasted_iota(jnp.int32, (lanes, lanes), 0)
     col_a = lax.broadcasted_iota(jnp.int32, (lanes, lanes), 1)
@@ -220,11 +254,11 @@
 
     for d in reversed(range(1, S)):
         own_q = low.at[me, pl.ds(0, kv)]
-        send(0, d, own_q, own_q, me, {"seq": flip(me, d)})
+        send(0, own_q, own_q, 0, peers[d])
     for c in range(H):
         own_kv = low.at[me, pl.ds(kv, 1)]
         target = hub(request, c)
-        send(2, c, own_kv, own_kv, me, {"seq": target}, target != me)
+        send(1, own_kv, own_kv, 1, target, target != me)
 
     for i in range(3, 7):
         loads[i].wait()
@@ -244,13 +278,11 @@
 
     lead = one_hot(lax.broadcasted_iota(jnp.int32, (lanes, hd), 1) == 0)
     row_s = lax.broadcasted_iota(jnp.int32, (16, lanes), 0)
-    for d in range(1, S):
-        source = flip(me, d)
-        arrive(0, source, low.at[source, pl.ds(0, kv)], {"seq": source})
+    arrive(0, low.at[pl.ds(0, S - 1), pl.ds(0, kv)])
 
     for r in range(R):
         for step in range(kv):
-            k = lax.rem(side + kv - 1 - step, kv)
+            k = turn(side, kv - 1 - step, kv)
             queries = low[pl.ds(r * G, G), k].reshape(lanes, hd)
             queries = jnp.concatenate([queries, lead], axis=1)
             scores = contract_last(ckeys[r, k], queries)
@@ -263,25 +295,18 @@
             stats = jnp.where(row_s == 1, coarse, jnp.where(row_s == 2, total - coarse, 0.0))
             stats = jnp.where(row_s == 0, high, stats).astype(BF16)
             for h in range(per_k):
-                part[r, k * per_k + h, :slab, :] = blend[h * slab : (h + 1) * slab].astype(BF16)
-                part[r, k * per_k + h, slab:, :] = stats
+                at = r * H + k * per_k + h
+                part[at, :slab, :] = blend[h * slab : (h + 1) * slab].astype(BF16)
+                part[at, slab:, :] = stats
             for d in reversed(range(per_k)):
-                c = k * per_k + lax.rem(lane_of + d, per_k)
+                c = k * per_k + turn(lane_of, d, per_k)
                 target = hub(r, c)
-                send(
-                    1,
-                    (r * kv + step) * per_k + d,
-                    part.at[r, c],
-                    gpart.at[me],
-                    me,
-                    {"seq": target},
-                    target != me,
-                )
+                send(2, part.at[r * H + c], gpart.at[me], 2, target, target != me)
 
     @pl.when(is_hub)
     def _():
-        k = lax.div(slot, per_k)
-        part_of = lax.rem(slot, per_k)
+        k = jnp.where(slot >= per_k, 1, 0) if kv == 2 else lax.div(slot, per_k)
+        part_of = slot - k * per_k
         ancestry = anc_ref[request].astype(F32).astype(BF16)
         spread = one_hot(
             lax.div(lax.broadcasted_iota(jnp.int32, (lanes, nodes), 0), g)
@@ -293,9 +318,7 @@
             == lax.broadcasted_iota(jnp.int32, (nodes, nodes), 1)
         )
         mask = contract_last(small, mask)
-        for d in range(1, G):
-            source = base + flip(place, d)
-            arrive(2, source, low.at[source, pl.ds(kv, 1)], {"seq": source})
+        arrive(1, low.at[pl.ds(0, G - 1), pl.ds(kv, 1)])
         form[kv, :lanes, :] = low[pl.ds(base, G), kv].reshape(lanes, hd).astype(F32)
         keys = form[kv, pl.ds(k, nodes, stride=g), :].astype(BF16)
         values = form[kv, pl.ds(kv + k, nodes, stride=g), :].astype(BF16)
@@ -307,10 +330,8 @@
         turned = contract_last(one_hot(row_a == col_a)[:hd, :hd], values).astype(BF16)
         wide[:hd] = jnp.dot(turned, mass.astype(BF16), preferred_element_type=F32)
         near = wide[pl.ds(pl.multiple_of(part_of * slab, slab), slab), :]
-        gpart[me] = part[request, slot]
-        for d in range(1, S):
-            source = flip(me, d)
-            arrive(1, source, gpart.at[source], {"seq": source})
+        gpart[me] = part[request * H + slot]
+        arrive(2, gpart.at[pl.ds(0, S - 1)])
         for s in range(S):
             tops[s * 16 : (s + 1) * 16] = gpart[s, slab:].astype(F32)
         highs = tops[pl.ds(0, S, stride=16), :]
@@ -322,11 +343,11 @@
         acc = near * late
         for s in range(S):
             acc = acc + gpart[s, :slab].astype(F32) * factors[s : s + 1]
-        heads[request, slot] = (acc * (1.0 / total)).astype(BF16)
+        heads[request * H + slot] = (acc * (1.0 / total)).astype(BF16)
 
     for d in reversed(range(1, S)):
-        done = heads.at[request, slot]
-        send(3, d, done, done, me, {"seq": flip(me, d)}, is_hub)
+        done = heads.at[request * H + slot]
+        send(3, done, done, at_heads + request * H + slot, peers[d], is_hub)
 
     entries = rkeys.shape[1]
     for i in range(7, 11):
@@ -354,14 +375,14 @@
 
     summed = None
     for step in range(kv):
-        k = lax.rem(side + step, kv)
+        k = turn(side, step, kv)
         lower = []
         for r in range(R):
             for d in range(per_k):
-                c = k * per_k + lax.rem(lane_of + d, per_k)
-                source = hub(r, c)
-                arrive(3, source, heads.at[r, c], {"seq": source}, source != me)
-            turned = heads[r, pl.ds(k * per_k, per_k)].reshape(hd, lanes)
+                c = k * per_k + turn(lane_of, d, per_k)
+                at = r * H + c
+                arrive(at_heads + at, heads.at[at], hub(r, c) != me)
+            turned = heads[pl.ds(r * H + k * per_k, per_k)].reshape(hd, lanes)
             turned = contract_last(order, turned).astype(BF16)
             lower.append(
                 jnp.concatenate(
@@ -386,14 +407,12 @@
                 terms[tp, p] = more.astype(BF16)
                 for d in reversed(range(1, T)):
                     mine = terms.at[tp, p]
-                    send(4, p * T + d, mine, mine, p * T + tp, {"tp": flip(tp, d)})
+                    send_twin(4, mine, mine, 3 + p, twins[d])
     loads[11].wait()
     loads[12].wait()
     residual = []
     for p in range(2):
-        for d in range(1, T):
-            source = flip(tp, d)
-            arrive(4, p * T + source, terms.at[source, p], {"tp": source})
+        arrive(3 + p, terms.at[pl.ds(0, T - 1), p])
         summed = terms[0, p].astype(F32)
         for t in range(1, T):
             summed = summed + terms[t, p].astype(F32)
@@ -408,45 +427,30 @@
         square[r] = squares[r * nodes : (r + 1) * nodes]
         for c in range(H):
             target = hub(r, c)
-            send(
-                9, r * H + c, square.at[r], gsquare.at[me], me, {"seq": target}, target != me
-            )
-    for copy in weights:
-        copy.wait()
+            send(5, square.at[r], gsquare.at[me], 5, target, target != me)
+    pltpu.make_async_copy(weight, weight, weight_sem).wait()
     scaled = (residual * gain_ref[...]).astype(BF16)
     for step in range(kv):
         for d in reversed(range(per_k)):
-            c = lax.rem(side + kv - 1 - step, kv) * per_k + lax.rem(lane_of + d, per_k)
+            c = turn(side, kv - 1 - step, kv) * per_k + turn(lane_of, d, per_k)
             out = jnp.dot(scaled, weight[c], preferred_element_type=F32).astype(BF16)
             for r in range(R):
-                proj[r, c] = out[r * nodes : (r + 1) * nodes]
+                proj[r * H + c] = out[r * nodes : (r + 1) * nodes]
                 target = hub(r, c)
-                send(
-                    5,
-                    (r * kv + step) * per_k + d,
-                    proj.at[r, c],
-                    gproj.at[me],
-                    me,
-                    {"seq": target},
-                    target != me,
-                )
+                send(6, proj.at[r * H + c], gproj.at[me], 6, target, target != me)
     res_ref[...] = residual
 
     @pl.when(is_hub)
     def _():
         gsquare[me] = square[request]
-        gproj[me] = proj[request, slot]
-        for d in range(1, S):
-            source = flip(me, d)
-            arrive(9, source, gsquare.at[source], {"seq": source})
+        gproj[me] = proj[request * H + slot]
+        arrive(5, gsquare.at[pl.ds(0, S - 1)])
         total = gsquare[0].astype(F32)
         for s in range(1, S):
             total = total + gsquare[s].astype(F32)
         total = total + pltpu.roll(total, hd // 2, 1)
         inverse = lax.rsqrt(total / width + norm_epsilon)
-        for d in range(1, S):
-            source = flip(me, d)
-            arrive(5, source, gproj.at[source], {"seq": source})
+        arrive(6, gproj.at[pl.ds(0, S - 1)])
         for t in range((qcols + kcols) // hd):
             at = slice(t * hd, (t + 1) * hd)
             total = gproj[0, :, at].astype(F32)
@@ -456,7 +460,7 @@
 
     for d in reversed(range(1, G)):
         mine = upper.at[slot]
-        send(6, d, mine, mine, me, {"seq": base + flip(place, d)}, is_hub)
+        send(7, mine, mine, at_upper + slot, base + mates[d], is_hub)
 
     spot = lax.broadcasted_iota(jnp.int32, (lanes, hd), 1)
     third = hd // 4
@@ -493,11 +497,10 @@
         return jnp.concatenate(tiles, axis=0)
 
     for step in range(kv):
-        k = lax.rem(side + step, kv)
+        k = turn(side, step, kv)
         for d in range(per_k):
-            c = k * per_k + lax.rem(lane_of + d, per_k)
-            source = hub(request, c)
-            arrive(6, source, upper.at[c], {"seq": source}, source != me)
+            c = k * per_k + turn(lane_of, d, per_k)
+            arrive(at_upper + c, upper.at[c], hub(request, c) != me)
         scores = contract_last(upper_queries(k), rkeys[k]) + bias_ref[k, 0:1, :]
         high = jnp.maximum(jnp.max(scores, axis=1, keepdims=True), lowest_high)
         mass = jnp.exp2((scores - high) * sharp).astype(BF16)
@@ -511,15 +514,8 @@
                     BF16
                 )
         for d in reversed(range(1, G)):
-            target = flip(place, d)
-            send(
-                7,
-                step * S + d,
-                upart.at[target, k],
-                ugpart.at[place, k],
-                step * S + place,
-                {"seq": base + target},
-            )
+            target = mates[d]
+            send(8, upart.at[target, k], ugpart.at[place, k], 7, base + target)
     ugpart[place] = upart[place]
 
     trees = []
@@ -532,11 +528,7 @@
         mass = jnp.exp2((scores - high) * sharp)
         total = jnp.sum(mass, axis=1, keepdims=True)
         trees.append((jnp.dot(mass.astype(BF16), values, preferred_element_type=F32), high, total))
-    for step in range(kv):
-        for d in range(1, G):
-            source = flip(place, d)
-            k = lax.rem(lax.div(source, G // 2) + step, kv)
-            arrive(7, step * S + source, ugpart.at[source, k], {"seq": base + source})
+    arrive(7, ugpart.at[pl.ds(0, G - 1)])
     for k in range(kv):
         blend, high, total = trees[k]
         stats = [unpack_stats(ugpart[s, k, rows:]) for s in range(G)]
@@ -553,11 +545,20 @@
         for j in range(g):
             h = k * g + j
             up_ref[:, h * hd : (h + 1) * hd] = form[k, pl.ds(j, own, stride=g), :]
-    for when, copy in sent:
-        if when is None:
-            copy.wait_send()
-        else:
-            pl.when(when)(copy.wait_send)
+    far = jnp.logical_not(is_hub)
+    gone(0, low.at[pl.ds(0, S - 1), pl.ds(0, kv)])
+    gone(1, low.at[pl.ds(0, H), pl.ds(kv, 1)], far)
+    gone(1, low.at[pl.ds(0, H - 1), pl.ds(kv, 1)], is_hub)
+    gone(2, part.at[pl.ds(0, R * H)], far)
+    gone(2, part.at[pl.ds(0, R * H - 1)], is_hub)
+    gone(3, heads.at[pl.ds(0, S - 1)], is_hub)
+    gone(4, terms.at[pl.ds(0, T - 1)])
+    gone(5, gsquare.at[pl.ds(0, R * H)], far)
+    gone(5, gsquare.at[pl.ds(0, R * H - 1)], is_hub)
+    gone(6, proj.at[pl.ds(0, R * H)], far)
+    gone(6, proj.at[pl.ds(0, R * H - 1)], is_hub)
+    gone(7, upper.at[pl.ds(0, G - 1)], is_hub)
+    gone(8, upart.at[pl.ds(0, G - 1)])
 
 
 def shards(
@@ -636,22 +637,22 @@
             pltpu.VMEM((kv, entries // kv, 2 * hd), BF16),
             pltpu.VMEM((kv, 8, entries // kv), F32),
             pltpu.VMEM((S, kv + 1, rows, hd), BF16),
-            pltpu.VMEM((R, H, slab + 16, lanes), BF16),
+            pltpu.VMEM((R * H, slab + 16, lanes), BF16),
             pltpu.VMEM((S, slab + 16, lanes), BF16),
             pltpu.VMEM((S * 16, lanes), F32),
-            pltpu.VMEM((R, H, slab, lanes), BF16),
+            pltpu.VMEM((S, slab, lanes), BF16),
             pltpu.VMEM((T, 2, M, features // 2), BF16),
-            pltpu.VMEM((R, H, nodes, cols), BF16),
+            pltpu.VMEM((R * H, nodes, cols), BF16),
             pltpu.VMEM((S, nodes, cols), BF16),
             pltpu.VMEM((R, nodes, hd), BF16),
             pltpu.VMEM((S, nodes, hd), BF16),
-            pltpu.VMEM((H, nodes, cols), BF16),
+            pltpu.VMEM((G, nodes, cols), BF16),
             pltpu.VMEM((G, kv, 2 * rows, hd), BF16),
             pltpu.VMEM((G, kv, 2 * rows, hd), BF16),
             pltpu.SemaphoreType.DMA((1 + len(big),)),
-            pltpu.SemaphoreType.DMA((H, 2)),
-            pltpu.SemaphoreType.DMA((10, 2 * max(S, T))),
-            pltpu.SemaphoreType.DMA((10, 2 * max(S, T))),
+            pltpu.SemaphoreType.DMA,
+            pltpu.SemaphoreType.DMA((9,)),
+            pltpu.SemaphoreType.DMA((8 + R * H + H,)),
         ],
         compiler_params=pltpu.CompilerParams(
             collective_id=0, has_side_effects=True, vmem_limit_bytes=56 * 1024 * 1024

time: 41.7 us -> 38.9 us (0.933)
  Pallas kernels: 40.2 us -> 37.4 us
    pallas_call x1, Pallas kernels: 39.6 us -> 36.8 us  [shards(): pl.pallas_call(functools.partial(kernel, (S, T, R, own, kv, g, hd)), out_...]
where the time goes in v2:
time: 38.9 us; the launch traced here: 38.7 us
  Pallas kernels  37.4 us (96%)
  between operations  1.29 us (3%)
    pallas_call x1, Pallas kernels, shards(): pl.pallas_call(functools.partial(kernel, (S, T, R, own, kv, g, hd)), out_...  36.8 us

profile of v2, /device:TPU:0, one launch (start us, length us, event | category | flops | bytes accessed | tf_op | source)
XLA Modules:
  0.0 38.7 jit_solution(18215459064851748313)
XLA Ops:
  1.3 36.8 %two_layers.1 = (f32[16,1024]{1,0:T(8,128)S(1)}, f32[2,2048]{1,0:T(2,128)S(1)}) custom-call(s32[1]{0:T(128)S(6)} %copy.18.lens_hbm, bf16[2,2048]{1,0:T(2,128)(2,1)} %q_hbm.1, bf16[2,256]{1,0:T(2,128)(2,1)} %k_hbm.1, bf16[2,256]{1,0:T(2,128)(2,1)} %v_hbm.1, bf16[1,2048,128]{2,1,0:T(8,128)(2,1)} %bitcast.8, bf16[1,2048,128]{2,1,0:T(8,128)(2,1)} %bitcast.9, ...), custom_call_target="tpu_custom_call" | custom-call | tf_op jit(solution)/shard_map/two_layers/pallas_call | solution.py:620
  38.0 0.6 %settle.1 = (f32[16,1024]{1,0:T(8,128)}, f32[2,2048]{1,0:T(2,128)}) custom-call(f32[16,1024]{1,0:T(8,128)S(1)} %get-tuple-element.4.a_ref, f32[2,2048]{1,0:T(2,128)S(1)} %get-tuple-element.5.b_ref), custom_call_target="tpu_custom_call" | custom-call | tf_op jit(solution)/shard_map/settle/pallas_call | solution.py:673
